TPU v7x, 32 devices: a whole 2x2x4 slice. The times are simulated.
32 devices in a mesh: shard: 8 (over z, core), rep: 4 (over y, x).
Axes of the slice: x: 2, y: 2, z: 4, core: 2. Of those that a mesh axis runs over, the one named last changes fastest.
Arguments:
- tokens: bfloat16 [12288, 5120], P(('shard', 'rep')), may hold values from -700 to 700
- norm_gain: float32 [5120], replicated, may hold values from 0.1 to 1.9
- key_bias: float32 [1024], replicated, may hold values from -4 to 4
- key_weight: bfloat16 [8192, 1024], P('shard'), may hold values from -0.078125 to 0.078125
- cotangent: bfloat16 [12288, 1024], P(('shard', 'rep')), may hold values from -40 to 40
- block_slot: int32 [40], replicated, may hold values from 0 to 63, as said below
Outputs:
- projected: bfloat16 [12288, 1024], P(('shard', 'rep'))
- token_grad: bfloat16 [12288, 5120], P(('shard', 'rep'))
- weight_grad: float32 [8192, 1024], P('shard')
- gain_grad: float32 [5120], replicated
- bias_grad: float32 [1024], replicated
Inputs may be any that keep to these rules, and one draw needn't show every extreme that they name: Entries are distinct; block b lies on the device of shard with index block_slot[b] // 8, at its local slot block_slot[b] % 8; in every draw some device holds 8 blocks.
All inputs are finite; a program needn't handle non-finite values.
Results may differ from a plain program's by a relative error of at most 0.013.
Values may be sent and summed in bfloat16 or wider, within the bound.
A program may use at most 128 MiB of HBM per device.

v0:
```python
import jax
import jax.numpy as jnp
from jax import lax
from jax.sharding import PartitionSpec as P

BLK = 128


EPS = 1e-06


def normalize(tokens, norm_gain):
    values = tokens.astype(jnp.float32)
    inv_rms = lax.rsqrt(jnp.mean(values * values, axis=-1, keepdims=True) + EPS)
    normed = (values * inv_rms * norm_gain).astype(jnp.bfloat16)
    return (values, inv_rms, normed)


def token_backward(values, inv_rms, grad_normed, norm_gain):
    scaled = grad_normed * norm_gain
    inner = jnp.mean(scaled * values, axis=-1, keepdims=True)
    return (inv_rms * (scaled - values * inv_rms * inv_rms * inner)).astype(jnp.bfloat16)


def local(tokens, norm_gain, key_bias, key_weight, cotangent, block_slot):
    values, inv_rms, normed = normalize(tokens, norm_gain)
    row_count = tokens.shape[0]
    width = tokens.shape[1]
    local_rows = key_weight.shape[0]
    shard_count = lax.axis_size("shard")
    replicas = lax.axis_size("rep")
    slot_total = shard_count * local_rows // BLK
    block_count = width // BLK
    block_of_slot = (
        jnp.full((slot_total,), -1, jnp.int32)
        .at[block_slot]
        .set(jnp.arange(block_count, dtype=jnp.int32))
    )
    present = block_of_slot >= 0
    normed_blocks = normed.reshape(row_count, block_count, BLK)
    normed_slots = jnp.take(normed_blocks, jnp.maximum(block_of_slot, 0), axis=1)
    normed_slots = jnp.where(present[None, :, None], normed_slots, jnp.zeros((), jnp.bfloat16))
    normed_slots = normed_slots.reshape(row_count, slot_total * BLK)
    piece = lax.all_gather(key_weight, "shard", axis=0, tiled=True)
    columns = normed_slots
    forward_sum = jnp.dot(columns, piece, preferred_element_type=jnp.float32)
    backward_part = lax.dot_general(
        cotangent, piece, (((1,), (1,)), ((), ())), preferred_element_type=jnp.float32
    )
    projected = (forward_sum + key_bias).astype(jnp.bfloat16)
    grad_normed = jnp.take(backward_part.reshape(row_count, slot_total, BLK), block_slot, axis=1)
    grad_normed = grad_normed.reshape(row_count, width)
    token_grad = token_backward(values, inv_rms, grad_normed, norm_gain)
    grad_scale = float(row_count * shard_count * replicas) ** (-0.5)
    columns = normed_slots
    group_sum = lax.psum_scatter(
        (
            lax.dot_general(
                columns, cotangent, (((0,), (0,)), ((), ())), preferred_element_type=jnp.float32
            )
            * grad_scale
        ).astype(jnp.bfloat16),
        "shard",
        scatter_dimension=0,
        tiled=True,
    ).astype(jnp.float32)
    gain_part = jnp.sum(grad_normed * values * inv_rms, axis=0) * grad_scale
    bias_part = jnp.sum(cotangent.astype(jnp.float32), axis=0) * grad_scale
    weight_grad = lax.psum(group_sum, "rep")
    gain_grad, bias_grad = lax.psum((gain_part, bias_part), ("shard", "rep"))
    return (projected, token_grad, weight_grad, gain_grad, bias_grad)


def solution(mesh):
    return jax.shard_map(
        local,
        mesh=mesh,
        in_specs=(
            P(("shard", "rep"), None),
            P(),
            P(),
            P("shard", None),
            P(("shard", "rep"), None),
            P(),
        ),
        out_specs=(
            P(("shard", "rep"), None),
            P(("shard", "rep"), None),
            P("shard", None),
            P(),
            P(),
        ),
        check_vma=False,
    )
```

profile of v0, /device:TPU:0, one launch (start us, length us, event | category | flops | bytes accessed | tf_op | source)
XLA Modules:
  0.0 577.4 jit_solution(7815864115164983269)
XLA Ops:
  7.2 0.0 copy-start.6
  7.2 0.0 copy-start.3
  7.2 0.0 all-gather.2.cloned.1.call-start
  7.2 0.7 all-gather.2.cloned.1.call-update
  7.9 0.0 reduce-scatter.2.cloned.1.call-start
  8.0 6.3 %copy.12 = bf16[384,5120]{0,1:T(8,128)(2,1)} copy(bf16[384,5120]{1,0:T(8,128)(2,1)} %param.6) | data formatting | bytes 7864320 | tf_op args[0]
  14.2 0.0 copy-done.6
  14.2 0.7 scatter_custom_fusion
  15.0 3.0 fusion.7
  18.1 0.1 broadcast_bitcast_fusion.2
  18.1 0.1 broadcast_bitcast_fusion
  18.2 145.2 %all-gather.2.cloned.1.call-done = bf16[8192,1024]{1,0:T(8,128)(2,1)} async-done(((bf16[1024,1024]{1,0:T(8,128)(2,1)}), bf16[8192,1024]{1,0:T(8,128)(2,1)}) %all-gather.2.cloned.1.call-update) | async-done | bytes 16777232 | tf_op jit(solution)/shard_map/all_gather | solution.py:44
  163.4 12.9 %convolution_bitcast_fusion = f32[48,64,8,128]{3,2,1,0:T(8,128)} fusion(bf16[384,1024]{1,0:T(8,128)(2,1)S(1)} %copy-done.3, bf16[8192,1024]{1,0:T(8,128)(2,1)} %all-gather.2.cloned.1.call-done), kind=kOutput, calls=%fused_computation.24 | convolution fusion | flops 6442450944 | bytes 30146560 | tf_op jit(solution)/shard_map/dot_general | solution.py:47
  176.3 10.8 %copy.20 = f32[48,64,8,128]{3,2,0,1:T(8,128)} copy(f32[48,64,8,128]{3,2,1,0:T(8,128)} %convolution_bitcast_fusion) | data formatting | bytes 25165824 | tf_op jit(solution)/shard_map/reshape | solution.py:51
  187.1 8.7 %gather_fusion.1 = f32[40,384,128]{2,1,0:T(8,128)} fusion(f32[384,64,128]{2,0,1:T(8,128)} %bitcast.34, s32[1024]{0:T(1024)S(1)} %pad_clamp_fusion), kind=kCustom, calls=%fused_computation.1 | custom fusion | bytes 15728800 | tf_op jit(solution)/shard_map/jit(_take)/gather | solution.py:51
  195.9 9.1 %copy.16 = f32[384,40,128]{0,2,1:T(8,128)} copy(f32[384,40,128]{2,0,1:T(8,128)} %bitcast.35) | data formatting | bytes 15728640 | tf_op jit(solution)/shard_map/jit(_take)/gather | solution.py:51
  205.0 8.8 %fusion.10 = (f32[5120]{0:T(1024)S(1)}, f32[384]{0:T(512)S(1)}) fusion(bf16[384,5120]{0,1:T(8,128)(2,1)} %copy.12, f32[384,40,128]{0,2,1:T(8,128)} %copy.16, f32[384]{0:T(512)S(1)} %add_rsqrt_fusion, pred[5120]{0:T(1024)(128)(4,1)S(1)} %broadcast_bitcast_fusion.2, f32[5120]{0:T(1024)S(1)} %copy-done.4), kind=kLoop, calls=%fused_computation.19 | loop fusion | flops 15723136 | bytes 11845632 | tf_op jit(solution)/shard_map/reduce_sum | solution.py:67
  213.8 5.5 fusion.6
  219.3 6.3 %copy.13 = bf16[384,40,128]{2,0,1:T(8,128)(2,1)} copy(bf16[384,40,128]{0,2,1:T(8,128)(2,1)} %bitcast.37) | data formatting | bytes 7864320 | tf_op jit(solution)/shard_map/reshape | solution.py:40
  225.5 6.1 %gather_fusion = bf16[64,384,128]{2,1,0:T(8,128)(2,1)} fusion(bf16[384,40,128]{2,0,1:T(8,128)(2,1)} %copy.13, s32[1024]{0:T(1024)S(1)} %pad_clamp_fusion.1), kind=kCustom, calls=%fused_computation | custom fusion | bytes 12583168 | tf_op jit(solution)/shard_map/jit(_take)/gather | solution.py:41
  231.7 8.6 %copy.14 = bf16[384,64,128]{0,2,1:T(8,128)(2,1)} copy(bf16[384,64,128]{2,0,1:T(8,128)(2,1)} %bitcast.36) | data formatting | bytes 12582912 | tf_op jit(solution)/shard_map/jit(_take)/gather | solution.py:41
  240.3 6.9 %fusion.12 = bf16[384,8192]{0,1:T(8,128)(2,1)S(1)} fusion(bf16[384,64,128]{0,2,1:T(8,128)(2,1)} %copy.14, pred[8192]{0:T(1024)(128)(4,1)S(1)} %get-tuple-element.18, pred[8192]{0:T(1024)(128)(4,1)S(1)} %get-tuple-element.19), kind=kLoop, calls=%fused_computation.23 | loop fusion | flops 6291456 | bytes 12599296 | tf_op jit(solution)/shard_map/jit(_where)/select_n | solution.py:42
  247.2 2.6 copy-done.2
  249.8 11.7 %multiply_convert_fusion = bf16[8192,1024]{1,0:T(8,128)(2,1)} fusion(bf16[384,8192]{0,1:T(8,128)(2,1)S(1)} %fusion.12, bf16[384,1024]{1,0:T(8,128)(2,1)S(1)} %copy-done.3), kind=kOutput, calls=%fused_computation.3 | convolution fusion | flops 6459228160 | bytes 23855104 | tf_op jit(solution)/shard_map/dot_general | solution.py:58
  261.4 0.0 reduce-scatter.2.cloned.1.call-update
  261.5 0.0 copy-start.5
  261.5 0.1 convert_reduce_fusion
  261.6 6.3 %copy.17 = bf16[384,5120]{1,0:T(8,128)(2,1)} copy(bf16[384,5120]{0,1:T(8,128)(2,1)} %get-tuple-element.14) | data formatting | bytes 7864320
  268.0 40.6 %all-reduce = (f32[5120]{0:T(1024)}, f32[1024]{0:T(1024)}) all-reduce(f32[5120]{0:T(1024)S(1)} %broadcast_multiply_fusion, f32[1024]{0:T(1024)S(1)} %broadcast_multiply_fusion.1), channel_id=1, replica_groups=mesh['shard'=8,'rep'=4] {'shard','rep'}, use_global_device_ids=true, to_apply=%region_6.7 | all-reduce | flops 6144 | bytes 49152 | tf_op jit(solution)/shard_map/psum | solution.py:70
  308.6 12.9 %add_convert_fusion = bf16[384,1024]{1,0:T(8,128)(2,1)} fusion(bf16[384,8192]{0,1:T(8,128)(2,1)} %copy-done.2, bf16[8192,1024]{1,0:T(8,128)(2,1)} %all-gather.2.cloned.1.call-done, f32[1024]{0:T(1024)S(1)} %copy-done.5), kind=kOutput, calls=%fused_computation.26 | convolution fusion | flops 6443237376 | bytes 23859200 | tf_op jit(solution)/shard_map/dot_general | solution.py:46
  321.5 107.6 %reduce-scatter.2.cloned.1.call-done = bf16[1024,1024]{1,0:T(8,128)(2,1)} async-done(((bf16[8192,1024]{1,0:T(8,128)(2,1)}), bf16[1024,1024]{1,0:T(8,128)(2,1)}) %reduce-scatter.2.cloned.1.call-update) | async-done | bytes 2097168 | tf_op jit(solution)/shard_map/reduce_scatter | solution.py:56
  429.0 141.5 %all-reduce.2 = f32[1024,1024]{1,0:T(8,128)} all-reduce(bf16[1024,1024]{1,0:T(8,128)(2,1)} %reduce-scatter.2.cloned.1.call-done), channel_id=1, replica_groups=mesh['shard'=8,'rep'=4] {'rep'}, use_global_device_ids=true, to_apply=%region_4.5 | all-reduce | flops 1048576 | bytes 6291456 | tf_op jit(solution)/shard_map/psum | solution.py:69
  (20 shorter events, 0.1 us)
Async XLA Ops:
  7.2 7.1 %copy-start.6 = (s32[40]{0:T(128)S(1)}, s32[40]{0:T(128)}, u32[]{:S(2)}) copy-start(s32[40]{0:T(128)} %param.11) | copy-start | bytes 484
  7.2 156.3 %copy-start.3 = (bf16[384,1024]{1,0:T(8,128)(2,1)S(1)}, bf16[384,1024]{1,0:T(8,128)(2,1)}, u32[]{:S(2)}) copy-start(bf16[384,1024]{1,0:T(8,128)(2,1)} %param.10) | copy-start | bytes 2359300
  7.2 156.2 %all-gather.2.cloned.1.call-start = ((), (), s32[]{:S(2)}) async-start(), calls=%async_computation.1 | async-start | bytes 18874368 | tf_op jit(solution)/shard_map/all_gather | solution.py:44
  7.9 421.1 %reduce-scatter.2.cloned.1.call-start = ((), (), s32[]{:S(2)}) async-start(), calls=%async_computation.2 | async-start | bytes 18874368 | tf_op jit(solution)/shard_map/reduce_scatter | solution.py:56
  195.9 9.1 %copy-start.4 = (f32[5120]{0:T(1024)S(1)}, f32[5120]{0:T(1024)}, u32[]{:S(2)}) copy-start(f32[5120]{0:T(1024)} %param.7) | copy-start | bytes 61444
  204.9 8.8 %copy-start = (f32[384,40,128]{0,2,1:T(8,128)S(1)}, f32[384,40,128]{0,2,1:T(8,128)}, u32[]{:S(2)}) copy-start(f32[384,40,128]{0,2,1:T(8,128)} %copy.16) | copy-start | bytes 23592964
  204.9 8.8 %copy-start.1 = (bf16[384,5120]{0,1:T(8,128)(2,1)S(1)}, bf16[384,5120]{0,1:T(8,128)(2,1)}, u32[]{:S(2)}) copy-start(bf16[384,5120]{0,1:T(8,128)(2,1)} %copy.12) | copy-start | bytes 11796484
  247.2 2.6 copy-start.2
  261.5 47.1 %copy-start.5 = (f32[1024]{0:T(1024)S(1)}, f32[1024]{0:T(1024)}, u32[]{:S(2)}) copy-start(f32[1024]{0:T(1024)} %param.8) | copy-start | bytes 12292
Sparse Core Ops, SparseCore 0:
  9.6 153.7 all-gather.1
  261.6 167.3 reduce-scatter.1
where the time goes:
time: 580 us; the launch traced here: 577 us
  waiting for transfers between devices  253 us (44%)
  blocking collectives  182 us (31%)
  local copies, waits for them, and re-layouts  65.7 us (11%)
  matrix products  37.4 us (6%)
  other arithmetic  24.4 us (4%)
  between operations  14.2 us (2%)
    all_gather x1, waiting for transfers between devices, local(): piece = lax.all_gather(key_weight, 'shard', axis=0, tiled=True)  145 us
    psum x1, blocking collectives, local(): weight_grad = lax.psum(group_sum, 'rep')  141 us
    reduce_scatter x1, waiting for transfers between devices, local(): lax.psum_scatter((lax.dot_general(columns, cotangent, (((0,), (0,)), ((),...  108 us
    psum x1, blocking collectives, local(): gain_grad, bias_grad = lax.psum((gain_part, bias_part), ('shard', 'rep'))  40.6 us
    gather x2, local copies, waits for them, and re-layouts, local(): jnp.take(backward_part.reshape(row_count, slot_total, BLK), block_slot, a...  17.8 us
    unnamed x16, local copies, waits for them, and re-layouts  15.2 us
    gather x2, local copies, waits for them, and re-layouts, local(): jnp.take(normed_blocks, jnp.maximum(block_of_slot, 0), axis=1)  14.7 us
    dot_general x1, matrix products, local(): forward_sum = jnp.dot(columns, piece, preferred_element_type=jnp.float32)  12.9 us
  transfers between devices with their start and end apart: 2, of which 2 were waited for; matrix products, arithmetic and copies ran while one was open for 5% of the time, Pallas kernels for 0%

commit v1 on v0

v1 whole, which is shorter than its diff:
```python
import functools
import jax
import jax.numpy as jnp
from jax import lax
from jax.experimental import pallas as pl
from jax.experimental.pallas import tpu as pltpu
from jax.sharding import PartitionSpec as P

BLK = 128
EPS = 1e-06
NJ = 4
SUB = BLK // NJ
QUAD = 4
MESH = pl.DeviceIdType.MESH
F32 = jnp.float32
BF16 = jnp.bfloat16


def comm_kernel(
    planes, cap, nblk, scale,
    tok, gain, cot, bos, w, whole, wgrad,
    inv, part, drecv, r1, r2, slots, zup, zdn, fin, frecv,
    loc_sem, agz_s, agz_r, agx_s, agx_r, agy_s, agy_r, agp_s, agp_r,
    d_s, d_r, r1_s, r1_r, r2_s, r2_r, zu_s, zu_r, zd_s, zd_r, f_s, f_r,
):
    s = lax.axis_index("shard")
    r = lax.axis_index("rep")
    z = s // 2
    c = s % 2
    quad = r % QUAD
    base = r - quad
    y = quad // 2
    x = quad % 2
    xq = y * 2 + (1 - x)
    yq = (1 - y) * 2 + x
    dq = (1 - y) * 2 + (1 - x)
    oc = 1 - c
    partner = (2 * z + oc, r)
    xdev = (s, base + xq)
    ydev = (s, base + yq)
    updev = (s + 2, r)
    dndev = (s - 2, r)
    plane = [(2 * z + oc, r)]
    for q in (xq, yq, dq):
        for cc in (c, oc):
            plane.append((2 * z + cc, base + q))
    has_up = z < planes - 1
    has_dn = z > 0

    bar = pltpu.get_barrier_semaphore()
    for dev in plane:
        pl.semaphore_signal(bar, inc=1, device_id=dev, device_id_type=MESH)

    @pl.when(has_up)
    def _():
        pl.semaphore_signal(bar, inc=1, device_id=updev, device_id_type=MESH)

    @pl.when(has_dn)
    def _():
        pl.semaphore_signal(bar, inc=1, device_id=dndev, device_id_type=MESH)

    pl.semaphore_wait(bar, 7 + has_up.astype(jnp.int32) + has_dn.astype(jnp.int32))

    def rdma(src, dst, ss, rs, dev):
        return pltpu.make_async_remote_copy(
            src_ref=src, dst_ref=dst, send_sem=ss, recv_sem=rs, device_id=dev, device_id_type=MESH
        )

    rows = w.shape[0]
    half = rows // 2
    quar = rows // 4
    hh = (x + y) % 2
    mine = pl.ds(hh * half, half)
    mine_x = pl.ds(hh * half, quar)
    mine_y = pl.ds(hh * half + quar, quar)
    other_x = pl.ds((1 - hh) * half, quar)
    other_y = pl.ds((1 - hh) * half + quar, quar)

    def own_z(d, dev):
        return rdma(w.at[mine], whole.at[s, mine], agz_s.at[d, z], agz_r.at[z], dev)

    def fwd_z(q, d, dev):
        ref = whole.at[2 * q + c, mine]
        return rdma(ref, ref, agz_s.at[d, q], agz_r.at[q], dev)

    def fwd_x(q):
        ref = whole.at[2 * q + c, mine_x]
        return rdma(ref, ref, agx_s.at[q], agx_r.at[q], xdev)

    def fwd_y(q):
        ref = whole.at[2 * q + c, mine_y]
        return rdma(ref, ref, agy_s.at[q], agy_r.at[q], ydev)

    def got_x(q):
        ref = whole.at[2 * q + c, other_x]
        return rdma(ref, ref, agx_s.at[q], agx_r.at[q], xdev)

    def got_y(q):
        ref = whole.at[2 * q + c, other_y]
        return rdma(ref, ref, agy_s.at[q], agy_r.at[q], ydev)

    def to_partner(i, q, rng):
        ref = whole.at[2 * q + c, rng]
        return rdma(ref, ref, agp_s.at[i, q], agp_r.at[i, q], partner)

    def from_partner(i, q, rng):
        ref = whole.at[2 * q + oc, rng]
        return rdma(ref, ref, agp_s.at[i, q], agp_r.at[i, q], partner)

    own_partner = rdma(w, whole.at[s], agp_s.at[0, z], agp_r.at[0, z], partner)
    own_local = pltpu.make_async_copy(w, whole.at[s], loc_sem)

    @pl.when(has_up)
    def _():
        own_z(0, updev).start()

    @pl.when(has_dn)
    def _():
        own_z(1, dndev).start()

    own_partner.start()
    own_local.start()

    def each_foreign(t, f):
        @pl.when(z - t >= 0)
        def _():
            f(z - t, 0)

        @pl.when(z + t < planes)
        def _():
            f(z + t, 1)

    def ag_arrive(t):
        def f(q, d):
            fwd_z(q, d, updev).wait_recv()
            if d == 0:
                @pl.when(has_up)
                def _():
                    fwd_z(q, 0, updev).start()
            else:
                @pl.when(has_dn)
                def _():
                    fwd_z(q, 1, dndev).start()
            fwd_x(q).start()
            fwd_y(q).start()
            to_partner(1, q, mine).start()

        each_foreign(t, f)

    def ag_side(t):
        def f(q, d):
            got_x(q).wait_recv()
            to_partner(2, q, other_x).start()
            got_y(q).wait_recv()
            to_partner(3, q, other_y).start()

        each_foreign(t, f)

    def ag_finish(t):
        def f(q, d):
            from_partner(1, q, mine).wait_recv()
            from_partner(2, q, other_x).wait_recv()
            from_partner(3, q, other_y).wait_recv()
            to_partner(1, q, mine).wait_send()
            to_partner(2, q, other_x).wait_send()
            to_partner(3, q, other_y).wait_send()
            fwd_x(q).wait_send()
            fwd_y(q).wait_send()
            if d == 0:
                @pl.when(has_up)
                def _():
                    fwd_z(q, 0, updev).wait_send()
            else:
                @pl.when(has_dn)
                def _():
                    fwd_z(q, 1, dndev).wait_send()

        each_foreign(t, f)

    tokens_here, width = tok.shape
    wide = 2 * BLK

    def squares(i, acc):
        v = tok[:, pl.ds(pl.multiple_of(i * wide, wide), wide)].astype(F32)
        v = v * v
        return acc + v[:, :BLK] + v[:, BLK:]

    acc = lax.fori_loop(0, width // wide, squares, jnp.zeros((tokens_here, BLK), F32))
    inv[...] = lax.rsqrt(jnp.sum(acc, axis=1, keepdims=True) / width + EPS)

    def term(i, carry):
        cols = pl.ds(pl.multiple_of(i * wide, wide), wide)
        normed = (tok[:, cols].astype(F32) * inv[...] * gain[:, cols]).astype(BF16)
        res = lax.dot_general(
            normed, cot[...], (((0,), (0,)), ((), ())), preferred_element_type=F32
        )
        res = (res * scale).astype(BF16)
        group = res.shape[1] // (2 * QUAD)
        for b in range(2):
            for j in range(NJ):
                lo = b * BLK + j * SUB
                for k in range(QUAD):
                    for cc in range(2):
                        col = (k * 2 + cc) * group
                        part[cc, j, k, i * 2 + b] = res[lo:lo + SUB, col:col + group]
        return carry

    lax.fori_loop(0, nblk // 2, term, 0)

    def d_copy(j):
        return rdma(part.at[oc, j], drecv.at[j], d_s.at[j], d_r.at[j], partner)

    for j in range(NJ):
        d_copy(j).start()

    def add_to(dst, src, count):
        step = 8

        def body(i, carry):
            sl = pl.ds(i * step, step)
            dst[sl] = (dst[sl].astype(F32) + src[sl].astype(F32)).astype(BF16)
            return carry

        lax.fori_loop(0, count // step, body, 0)

    def first_hop(j):
        near, dev = (xq, xdev) if j % 2 == 0 else (yq, ydev)
        return (
            rdma(part.at[c, j, near], r1.at[j, 0], r1_s.at[j, 0], r1_r.at[j, 0], dev),
            rdma(part.at[c, j, dq], r1.at[j, 1], r1_s.at[j, 1], r1_r.at[j, 1], dev),
        )

    def second_hop(j):
        far, dev = (yq, ydev) if j % 2 == 0 else (xq, xdev)
        return rdma(part.at[c, j, far], r2.at[j], r2_s.at[j], r2_r.at[j], dev)

    for j in range(NJ):
        d_copy(j).wait()
        near, far = (xq, yq) if j % 2 == 0 else (yq, xq)
        hops = first_hop(j)
        add_to(part.at[c, j, dq], drecv.at[j, dq], nblk)
        add_to(part.at[c, j, near], drecv.at[j, near], nblk)
        hops[1].start()
        hops[0].start()
        add_to(part.at[c, j, far], drecv.at[j, far], nblk)
        add_to(part.at[c, j, quad], drecv.at[j, quad], nblk)

    ag_arrive(1)
    for j in range(NJ):
        hops = first_hop(j)
        far = yq if j % 2 == 0 else xq
        hops[1].wait_recv()
        add_to(part.at[c, j, far], r1.at[j, 1], nblk)
        second_hop(j).start()
        hops[0].wait_recv()
        add_to(part.at[c, j, quad], r1.at[j, 0], nblk)

    per_plane = 2 * cap

    def z_copy(buf, ss, rs, j, q, dev):
        return rdma(slots.at[j, q], buf.at[j, q], ss.at[j, q], rs.at[j, q], dev)

    def up_copy(j, q):
        return z_copy(zup, zu_s, zu_r, j, q, updev)

    def dn_copy(j, q):
        return z_copy(zdn, zd_s, zd_r, j, q, dndev)

    def place(j):
        second_hop(j).wait_recv()
        add_to(part.at[c, j, quad], r2.at[j], nblk)

        def body(i, carry):
            for u in range(per_plane):
                b = bos[i * per_plane + u]
                val = part[c, j, quad, jnp.maximum(b, 0)]
                slots[j, i, u] = jnp.where(b >= 0, val.astype(F32), 0.0).astype(BF16)
            return carry

        lax.fori_loop(0, planes, body, 0)

    def z_step(j, t):
        qu = planes - 1 - t

        @pl.when(z < qu)
        def _():
            @pl.when(has_dn)
            def _():
                up_copy(j, qu).wait_recv()
                add_to(slots.at[j, qu], zup.at[j, qu], per_plane)

            up_copy(j, qu).start()

        @pl.when(z > t)
        def _():
            @pl.when(has_up)
            def _():
                dn_copy(j, t).wait_recv()
                add_to(slots.at[j, t], zdn.at[j, t], per_plane)

            dn_copy(j, t).start()

    my_id = quad * 2 + c

    def f_copies(j):
        out = []
        for n, dev in enumerate(plane):
            cc = oc if n % 2 == 0 else c
            out.append(
                rdma(
                    fin.at[j, pl.ds(cc * cap, cap)], frecv.at[my_id, j],
                    f_s.at[j, n], f_r.at[j, my_id], dev,
                )
            )
        return out

    def z_end(j):
        @pl.when(has_dn)
        def _():
            up_copy(j, z).wait_recv()
            add_to(slots.at[j, z], zup.at[j, z], per_plane)

        @pl.when(has_up)
        def _():
            dn_copy(j, z).wait_recv()
            add_to(slots.at[j, z], zdn.at[j, z], per_plane)

        fin[j] = slots[j, z]
        frecv[my_id, j] = slots[j, z, pl.ds(c * cap, cap)]
        for cp in f_copies(j):
            cp.start()

    for t in range(2, planes):
        ag_side(t - 1)
        ag_arrive(t)
    for j in range(NJ):
        place(j)
        for t in range(planes - 1):
            z_step(j, t)
    ag_side(planes - 1)
    for j in range(NJ):
        z_end(j)

    def f_got(j, n):
        ids = [quad * 2 + oc]
        for q in (xq, yq, dq):
            ids += [q * 2 + c, q * 2 + oc]
        sender = ids[n]
        return rdma(
            fin.at[j, pl.ds(0, cap)], frecv.at[sender, j],
            f_s.at[j, n], f_r.at[j, sender], plane[n],
        )

    for j in range(NJ):
        for n in range(7):
            f_got(j, n).wait_recv()

        def body(u, carry):
            for n in range(8):
                wgrad[pl.ds(pl.multiple_of(u * BLK + j * SUB, SUB), SUB), n * BLK:(n + 1) * BLK] = (
                    frecv[n, j, u].astype(F32)
                )
            return carry

        lax.fori_loop(0, cap, body, 0)

    for j in range(NJ):
        for cp in first_hop(j):
            cp.wait_send()
        second_hop(j).wait_send()
        for cp in f_copies(j):
            cp.wait_send()
        for t in range(planes - 1):
            @pl.when(z < planes - 1 - t)
            def _():
                up_copy(j, planes - 1 - t).wait_send()

            @pl.when(z > t)
            def _():
                dn_copy(j, t).wait_send()

    for t in range(1, planes):
        ag_finish(t)
    own_partner.wait_send()
    from_partner_own = rdma(w, whole.at[2 * z + oc], agp_s.at[0, z], agp_r.at[0, z], partner)
    from_partner_own.wait_recv()
    own_local.wait()

    @pl.when(has_up)
    def _():
        own_z(0, updev).wait_send()

    @pl.when(has_dn)
    def _():
        own_z(1, dndev).wait_send()


def communicate(tokens, norm_gain, cotangent, block_of_slot, key_weight, scale):
    shard_count = lax.axis_size("shard")
    planes = shard_count // 2
    rows, cols = key_weight.shape
    cap = rows // BLK
    width = tokens.shape[1]
    nblk = width // BLK
    group = cols // (2 * QUAD)
    dma = pltpu.SemaphoreType.DMA
    vm = pltpu.VMEM
    return pl.pallas_call(
        functools.partial(comm_kernel, planes, cap, nblk, scale),
        out_shape=(
            jax.ShapeDtypeStruct((shard_count, rows, cols), BF16),
            jax.ShapeDtypeStruct((rows, cols), F32),
        ),
        in_specs=[
            pl.BlockSpec(memory_space=vm),
            pl.BlockSpec(memory_space=vm),
            pl.BlockSpec(memory_space=vm),
            pl.BlockSpec(memory_space=pltpu.SMEM),
            pl.BlockSpec(memory_space=vm),
        ],
        out_specs=(pl.BlockSpec(memory_space=pl.ANY), pl.BlockSpec(memory_space=vm)),
        scratch_shapes=[
            vm((tokens.shape[0], 1), F32),
            vm((2, NJ, QUAD, nblk, SUB, group), BF16),
            vm((NJ, QUAD, nblk, SUB, group), BF16),
            vm((NJ, 2, nblk, SUB, group), BF16),
            vm((NJ, nblk, SUB, group), BF16),
            vm((NJ, planes, 2 * cap, SUB, group), BF16),
            vm((NJ, planes, 2 * cap, SUB, group), BF16),
            vm((NJ, planes, 2 * cap, SUB, group), BF16),
            vm((NJ, 2 * cap, SUB, group), BF16),
            vm((2 * QUAD, NJ, cap, SUB, group), BF16),
            dma(()),
            dma((2, planes)), dma((planes,)),
            dma((planes,)), dma((planes,)),
            dma((planes,)), dma((planes,)),
            dma((4, planes)), dma((4, planes)),
            dma((NJ,)), dma((NJ,)),
            dma((NJ, 2)), dma((NJ, 2)),
            dma((NJ,)), dma((NJ,)),
            dma((NJ, planes)), dma((NJ, planes)),
            dma((NJ, planes)), dma((NJ, planes)),
            dma((NJ, 7)), dma((NJ, 8)),
        ],
        compiler_params=pltpu.CompilerParams(
            collective_id=0, has_side_effects=True, vmem_limit_bytes=60 * 1024 * 1024
        ),
    )(tokens, norm_gain[None, :], cotangent, block_of_slot, key_weight)


def local(tokens, norm_gain, key_bias, key_weight, cotangent, block_slot):
    row_count, width = tokens.shape
    shard_count = lax.axis_size("shard")
    replicas = lax.axis_size("rep")
    cap = key_weight.shape[0] // BLK
    slot_total = shard_count * cap
    block_count = width // BLK
    grad_scale = float(row_count * shard_count * replicas) ** (-0.5)
    match = block_slot[None, :] == jnp.arange(slot_total, dtype=jnp.int32)[:, None]
    numbers = jnp.arange(1, block_count + 1, dtype=jnp.int32)[None, :]
    block_of_slot = jnp.sum(jnp.where(match, numbers, 0), axis=1) - 1
    whole, weight_grad = communicate(
        tokens, norm_gain, cotangent, block_of_slot, key_weight, grad_scale
    )
    if replicas > QUAD:
        groups = [list(range(i, replicas, QUAD)) for i in range(QUAD)]
        weight_grad = lax.psum(weight_grad, "rep", axis_index_groups=groups)
    weight = jnp.take(whole.reshape(slot_total, BLK, -1), block_slot, axis=0)
    weight = weight.reshape(width, -1)
    values = tokens.astype(F32)
    inv_rms = lax.rsqrt(jnp.mean(values * values, axis=-1, keepdims=True) + EPS)
    normed = (values * inv_rms * norm_gain).astype(BF16)
    projected = jnp.dot(normed, weight, preferred_element_type=F32) + key_bias
    projected = projected.astype(BF16)
    grad_normed = lax.dot_general(
        cotangent, weight, (((1,), (1,)), ((), ())), preferred_element_type=F32
    )
    scaled = grad_normed * norm_gain
    inner = jnp.mean(scaled * values, axis=-1, keepdims=True)
    token_grad = (inv_rms * (scaled - values * inv_rms * inv_rms * inner)).astype(BF16)
    gain_part = jnp.sum(grad_normed * values * inv_rms, axis=0) * grad_scale
    bias_part = jnp.sum(cotangent.astype(F32), axis=0) * grad_scale
    gain_grad, bias_grad = lax.psum((gain_part, bias_part), ("shard", "rep"))
    return (projected, token_grad, weight_grad, gain_grad, bias_grad)


def solution(mesh):
    return jax.shard_map(
        local,
        mesh=mesh,
        in_specs=(
            P(("shard", "rep"), None),
            P(),
            P(),
            P("shard", None),
            P(("shard", "rep"), None),
            P(),
        ),
        out_specs=(
            P(("shard", "rep"), None),
            P(("shard", "rep"), None),
            P("shard", None),
            P(),
            P(),
        ),
        check_vma=False,
    )
```

time: 580 us -> 273 us (0.47)
  waiting for transfers between devices: 253 us -> 0 us
  Pallas kernels: 0 us -> 159 us
  blocking collectives: 182 us -> 47.1 us
  local copies, waits for them, and re-layouts: 65.7 us -> 29 us
  matrix products: 37.4 us -> 17.2 us
  between operations: 14.2 us -> 0.74 us
    pallas_call x0 -> x1, Pallas kernels: none -> 159 us  [communicate(): pl.pallas_call(functools.partial(comm_kernel, planes, cap, nblk, scale),...]
    all_gather x1 -> x0, waiting for transfers between devices: 145 us -> none  [local(): piece = lax.all_gather(key_weight, 'shard', axis=0, tiled=True)]
    psum x1 -> x0, blocking collectives: 141 us -> none  [local(): weight_grad = lax.psum(group_sum, 'rep')]
    reduce_scatter x1 -> x0, waiting for transfers between devices: 108 us -> none  [local(): lax.psum_scatter((lax.dot_general(columns, cotangent, (((0,), (0,)), ((),...]
    gather x4 -> x1, local copies, waits for them, and re-layouts: 32.6 us -> 11.6 us  [local(): weight = jnp.take(whole.reshape(slot_total, BLK, -1), block_slot, axis=0)]
    dot_general x3 -> x2, matrix products: 37.4 us -> 17.2 us  [the longest x1 10.5 us: local(): projected = jnp.dot(normed, weight, preferred_element_type=F32) + key_bias]
    reshape x2 -> x0, local copies, waits for them, and re-layouts: 17.1 us -> none  [the longest x1 10.8 us: local(): backward_part.reshape(row_count, slot_total, BLK)]
    reduce_sum x3, other arithmetic: 12 us -> 4.07 us  [the longest x1 3.18 us: local(): inv_rms = lax.rsqrt(jnp.mean(values * values, axis=-1, keepdims=True) + EPS)]
  transfers between devices with their start and end apart: 2 -> 0, of which waited for: 2 -> 0; matrix products, arithmetic and copies ran while one was open for 5% -> 0% of each run, Pallas kernels for 0% -> 0%
where the time goes in v1:
time: 273 us; the launch traced here: 272 us
  Pallas kernels  159 us (58%)
  blocking collectives  47.1 us (17%)
  local copies, waits for them, and re-layouts  29 us (11%)
  other arithmetic  19.4 us (7%)
  matrix products  17.2 us (6%)
    pallas_call x1, Pallas kernels, communicate(): pl.pallas_call(functools.partial(comm_kernel, planes, cap, nblk, scale),...  159 us
    psum x1, blocking collectives, local(): gain_grad, bias_grad = lax.psum((gain_part, bias_part), ('shard', 'rep'))  47.1 us
    unnamed x19, local copies, waits for them, and re-layouts  17.4 us
    gather x1, local copies, waits for them, and re-layouts, local(): weight = jnp.take(whole.reshape(slot_total, BLK, -1), block_slot, axis=0)  11.6 us
    select_n x2, other arithmetic, local(): weight = jnp.take(whole.reshape(slot_total, BLK, -1), block_slot, axis=0)  10.8 us
    dot_general x1, matrix products, local(): projected = jnp.dot(normed, weight, preferred_element_type=F32) + key_bias  10.5 us
    dot_general x1, matrix products, local(): lax.dot_general(cotangent, weight, (((1,), (1,)), ((), ())), preferred_el...  6.66 us

profile of v1, /device:TPU:0, one launch (start us, length us, event | category | flops | bytes accessed | tf_op | source)
XLA Modules:
  0.0 272.3 jit_solution(7719671821782388824)
XLA Ops:
  0.6 0.7 select_reduce_fusion
  1.4 0.5 broadcast_add_fusion.bos
  1.9 159.0 %shard_map.101 = (bf16[8,1024,1024]{2,1,0:T(8,128)(2,1)}, f32[1024,1024]{1,0:T(8,128)}) custom-call(bf16[384,5120]{1,0:T(8,128)(2,1)} %tok.1, f32[1,5120]{1,0:T(1,128)} %bitcast.19, bf16[384,1024]{1,0:T(8,128)(2,1)} %cot.1, s32[64]{0:T(128)} %broadcast_add_fusion.bos, bf16[1024,1024]{1,0:T(8,128)(2,1)} %w.1), custom_call_target="tpu_custom_call" | custom-call | tf_op jit(solution)/shard_map/pallas_call | solution.py:408
  160.9 0.7 compare_select_fusion
  161.5 0.0 copy-start.4
  161.5 11.6 %gather_fusion = bf16[40,128,1024]{2,1,0:T(8,128)(2,1)} fusion(bf16[64,128,1024]{2,1,0:T(8,128)(2,1)} %bitcast.18, s32[1024]{0:T(1024)S(1)} %pad_clamp_fusion), kind=kCustom, calls=%fused_computation | custom fusion | bytes 20971680 | tf_op jit(solution)/shard_map/jit(_take)/gather | solution.py:468
  173.1 0.0 copy-done.4
  173.1 0.1 broadcast_bitcast_fusion
  173.2 10.2 %bitcast_select_fusion = bf16[5120,1024]{1,0:T(8,128)(2,1)} fusion(bf16[40,128,1024]{2,1,0:T(8,128)(2,1)} %gather_fusion, pred[5120]{0:T(1024)(128)(4,1)S(1)} %broadcast_bitcast_fusion), kind=kLoop, calls=%fused_computation.5 | loop fusion | flops 5242880 | bytes 20976640 | tf_op jit(solution)/shard_map/jit(_take)/select_n | solution.py:468
  183.4 0.0 copy-start.2
  183.4 0.0 copy-start.3
  183.4 6.3 %copy.13 = bf16[384,5120]{0,1:T(8,128)(2,1)} copy(bf16[384,5120]{1,0:T(8,128)(2,1)} %tok.1) | data formatting | bytes 7864320 | tf_op args[0]
  189.7 0.0 slice-start
  189.7 3.2 %fusion.7 = f32[384]{0:T(512)S(1)} fusion(bf16[384,5120]{0,1:T(8,128)(2,1)} %copy.13), kind=kLoop, calls=%fused_computation.13 | loop fusion | flops 5897856 | bytes 3933696 | tf_op jit(solution)/shard_map/reduce_sum | solution.py:471
  192.9 0.0 copy-done.2
  192.9 0.0 copy-done.3
  192.9 0.0 copy-start
  192.9 0.0 slice-start.1
  192.9 0.0 slice-start.2
  192.9 0.0 copy-start.1
  192.9 10.5 %add_convert_fusion = bf16[384,1024]{1,0:T(8,128)(2,1)} fusion(bf16[5120,1024]{1,0:T(8,128)(2,1)} %bitcast_select_fusion, bf16[384,5120]{0,1:T(8,128)(2,1)} %copy.13, f32[5120]{0:T(1024)S(1)} %copy-done.2, f32[384]{0:T(512)S(1)} %add_rsqrt_fusion, f32[1024]{0:T(1024)S(1)} %copy-done.3), kind=kOutput, calls=%fused_computation.22 | convolution fusion | flops 4035182592 | bytes 15230464 | tf_op jit(solution)/shard_map/dot_general | solution.py:473
  203.4 0.0 slice-done
  203.4 0.0 copy-done
  203.4 0.0 slice-done.1
  203.4 0.0 slice-done.2
  203.5 0.0 copy-done.1
  203.5 6.7 %fusion.10 = (f32[5120]{0:T(1024)S(1)}, f32[384]{0:T(512)S(1)}, f32[5120,384]{1,0:T(8,128)S(1)}) fusion(bf16[384,5120]{0,1:T(8,128)(2,1)S(1)} %copy-done, f32[384]{0:T(512)S(1)} %add_rsqrt_fusion, f32[5120]{0:T(1024)S(1)} %copy-done.2, bf16[5120,1024]{1,0:T(8,128)(2,1)S(1)} %bitcast.17, bf16[384,1024]{1,0:T(8,128)(2,1)S(1)} %copy-done.1), kind=kOutput, calls=%fused_computation.16 | convolution fusion | flops 4040288768 | bytes 23112704 | tf_op jit(solution)/shard_map/dot_general | solution.py:475
  210.1 3.9 %fusion.6 = bf16[384,5120]{0,1:T(8,128)(2,1)} fusion(bf16[384,5120]{0,1:T(8,128)(2,1)S(1)} %copy-done, f32[5120,384]{1,0:T(8,128)S(1)} %get-tuple-element.23, f32[384]{0:T(512)S(1)} %broadcast_multiply_fusion.2, f32[5120]{0:T(1024)S(1)} %copy-done.2, f32[384]{0:T(512)S(1)} %add_rsqrt_fusion), kind=kLoop, calls=%fused_computation.12 | loop fusion | flops 15728640 | bytes 15752192 | tf_op jit(solution)/shard_map/convert_element_type | solution.py:480
  214.1 6.3 %copy.14 = bf16[384,5120]{1,0:T(8,128)(2,1)} copy(bf16[384,5120]{0,1:T(8,128)(2,1)} %fusion.6) | data formatting | bytes 7864320
  220.3 0.1 convert_reduce_fusion
  220.5 47.1 %all-reduce = (f32[5120]{0:T(1024)}, f32[1024]{0:T(1024)}) all-reduce(f32[5120]{0:T(1024)S(1)} %broadcast_multiply_fusion, f32[1024]{0:T(1024)S(1)} %broadcast_multiply_fusion.1), channel_id=1, replica_groups=mesh['shard'=8,'rep'=4] {'shard','rep'}, use_global_device_ids=true, to_apply=%region_4.5 | all-reduce | flops 6144 | bytes 49152 | tf_op jit(solution)/shard_map/psum | solution.py:483
  267.5 4.8 %copy.16 = f32[1024,1024]{1,0:T(8,128)} copy(f32[1024,1024]{1,0:T(8,128)} %get-tuple-element.31) | data formatting | bytes 8388608
  (8 shorter events, 0.0 us)
Async XLA Ops:
  161.5 11.6 %copy-start.4 = (s32[40]{0:T(128)S(1)}, s32[40]{0:T(128)}, u32[]{:S(2)}) copy-start(s32[40]{0:T(128)} %param.11) | copy-start | bytes 484
  183.4 9.5 %copy-start.2 = (f32[5120]{0:T(1024)S(1)}, f32[5120]{0:T(1024)}, u32[]{:S(2)}) copy-start(f32[5120]{0:T(1024)} %param.7) | copy-start | bytes 61444
  183.4 9.5 %copy-start.3 = (f32[1024]{0:T(1024)S(1)}, f32[1024]{0:T(1024)}, u32[]{:S(2)}) copy-start(f32[1024]{0:T(1024)} %param.8) | copy-start | bytes 12292
  189.7 13.8 %slice-start = ((s8[10485760]{0:T(1024)(128)(4,1)}), s8[4194304]{0:T(1024)(128)(4,1)S(1)}, s32[]{:S(2)}) async-start(s8[10485760]{0:T(1024)(128)(4,1)} %bitcast.16), calls=%async_computation | async-start | bytes 8388608
  192.9 10.6 %copy-start = (bf16[384,5120]{0,1:T(8,128)(2,1)S(1)}, bf16[384,5120]{0,1:T(8,128)(2,1)}, u32[]{:S(2)}) copy-start(bf16[384,5120]{0,1:T(8,128)(2,1)} %copy.13) | copy-start | bytes 11796484
  192.9 10.6 %slice-start.1 = ((s8[10485760]{0:T(1024)(128)(4,1)}), s8[4194304]{0:T(1024)(128)(4,1)S(1)}, s32[]{:S(2)}) async-start(s8[10485760]{0:T(1024)(128)(4,1)} %bitcast.16), calls=%async_computation.1 | async-start | bytes 8388608
  192.9 10.5 %slice-start.2 = ((s8[10485760]{0:T(1024)(128)(4,1)}), s8[2097152]{0:T(1024)(128)(4,1)S(1)}, s32[]{:S(2)}) async-start(s8[10485760]{0:T(1024)(128)(4,1)} %bitcast.16), calls=%async_computation.2 | async-start | bytes 4194304
  192.9 10.5 %copy-start.1 = (bf16[384,1024]{1,0:T(8,128)(2,1)S(1)}, bf16[384,1024]{1,0:T(8,128)(2,1)}, u32[]{:S(2)}) copy-start(bf16[384,1024]{1,0:T(8,128)(2,1)} %cot.1) | copy-start | bytes 2359300

commit v2 on v1

--- a/solution.py
+++ b/solution.py
@@ -18,10 +18,10 @@
 
 def comm_kernel(
     planes, cap, nblk, scale,
-    tok, gain, cot, bos, w, whole, wgrad,
-    inv, part, drecv, r1, r2, slots, zup, zdn, fin, frecv,
+    tok, gain, cot, bias, bos, slot_of, w, proj, tgrad, wgrad, vec,
+    whole, inv, coef, fwd, gst, grecv, gz, part, drecv, r1, r2, slots, zup, zdn, fin, frecv,
     loc_sem, agz_s, agz_r, agx_s, agx_r, agy_s, agy_r, agp_s, agp_r,
-    d_s, d_r, r1_s, r1_r, r2_s, r2_r, zu_s, zu_r, zd_s, zd_r, f_s, f_r,
+    d_s, d_r, r1_s, r1_r, r2_s, r2_r, zu_s, zu_r, zd_s, zd_r, f_s, f_r, g_s, g_r, gz_s, gz_r,
 ):
     s = lax.axis_index("shard")
     r = lax.axis_index("rep")
@@ -51,64 +51,62 @@
     for dev in plane:
         pl.semaphore_signal(bar, inc=1, device_id=dev, device_id_type=MESH)
 
-    @pl.when(has_up)
-    def _():
-        pl.semaphore_signal(bar, inc=1, device_id=updev, device_id_type=MESH)
-
-    @pl.when(has_dn)
-    def _():
-        pl.semaphore_signal(bar, inc=1, device_id=dndev, device_id_type=MESH)
-
-    pl.semaphore_wait(bar, 7 + has_up.astype(jnp.int32) + has_dn.astype(jnp.int32))
+    others = [(2 * ((z + d) % planes) + c, r) for d in range(1, planes)]
+    for dev in others:
+        pl.semaphore_signal(bar, inc=1, device_id=dev, device_id_type=MESH)
+    pl.semaphore_wait(bar, 7 + planes - 1)
 
     def rdma(src, dst, ss, rs, dev):
         return pltpu.make_async_remote_copy(
             src_ref=src, dst_ref=dst, send_sem=ss, recv_sem=rs, device_id=dev, device_id_type=MESH
         )
 
-    rows = w.shape[0]
-    half = rows // 2
-    quar = rows // 4
+    half = cap // 2
+    quar = cap // 4
     hh = (x + y) % 2
-    mine = pl.ds(hh * half, half)
-    mine_x = pl.ds(hh * half, quar)
-    mine_y = pl.ds(hh * half + quar, quar)
-    other_x = pl.ds((1 - hh) * half, quar)
-    other_y = pl.ds((1 - hh) * half + quar, quar)
+
+    def span(shard, start, size):
+        return whole.at[pl.ds(shard * cap + start, size)]
+
+    mine = (hh * half, half)
+    mine_x = (hh * half, quar)
+    mine_y = (hh * half + quar, quar)
+    other_x = ((1 - hh) * half, quar)
+    other_y = ((1 - hh) * half + quar, quar)
 
     def own_z(d, dev):
-        return rdma(w.at[mine], whole.at[s, mine], agz_s.at[d, z], agz_r.at[z], dev)
+        return rdma(w.at[pl.ds(*mine)], span(s, *mine), agz_s.at[d, z], agz_r.at[z], dev)
 
     def fwd_z(q, d, dev):
-        ref = whole.at[2 * q + c, mine]
+        ref = span(2 * q + c, *mine)
         return rdma(ref, ref, agz_s.at[d, q], agz_r.at[q], dev)
 
     def fwd_x(q):
-        ref = whole.at[2 * q + c, mine_x]
+        ref = span(2 * q + c, *mine_x)
         return rdma(ref, ref, agx_s.at[q], agx_r.at[q], xdev)
 
     def fwd_y(q):
-        ref = whole.at[2 * q + c, mine_y]
+        ref = span(2 * q + c, *mine_y)
         return rdma(ref, ref, agy_s.at[q], agy_r.at[q], ydev)
 
     def got_x(q):
-        ref = whole.at[2 * q + c, other_x]
+        ref = span(2 * q + c, *other_x)
         return rdma(ref, ref, agx_s.at[q], agx_r.at[q], xdev)
 
     def got_y(q):
-        ref = whole.at[2 * q + c, other_y]
+        ref = span(2 * q + c, *other_y)
         return rdma(ref, ref, agy_s.at[q], agy_r.at[q], ydev)
 
     def to_partner(i, q, rng):
-        ref = whole.at[2 * q + c, rng]
+        ref = span(2 * q + c, *rng)
         return rdma(ref, ref, agp_s.at[i, q], agp_r.at[i, q], partner)
 
     def from_partner(i, q, rng):
-        ref = whole.at[2 * q + oc, rng]
+        ref = span(2 * q + oc, *rng)
         return rdma(ref, ref, agp_s.at[i, q], agp_r.at[i, q], partner)
 
-    own_partner = rdma(w, whole.at[s], agp_s.at[0, z], agp_r.at[0, z], partner)
-    own_local = pltpu.make_async_copy(w, whole.at[s], loc_sem)
+    own_partner = rdma(w, span(s, 0, cap), agp_s.at[0, z], agp_r.at[0, z], partner)
+    own_local = pltpu.make_async_copy(w, span(s, 0, cap), loc_sem)
 
     @pl.when(has_up)
     def _():
@@ -205,13 +203,19 @@
                         part[cc, j, k, i * 2 + b] = res[lo:lo + SUB, col:col + group]
         return carry
 
-    lax.fori_loop(0, nblk // 2, term, 0)
-
-    def d_copy(j):
-        return rdma(part.at[oc, j], drecv.at[j], d_s.at[j], d_r.at[j], partner)
-
-    for j in range(NJ):
-        d_copy(j).start()
+
+    hb = nblk // 2
+
+    def d_copy(j, i):
+        blocks = pl.ds(i * hb, hb)
+        return rdma(
+            part.at[oc, j, :, blocks], drecv.at[j, :, blocks], d_s.at[j, i], d_r.at[j, i], partner
+        )
+
+    for i in range(2):
+        lax.fori_loop(i * hb // 2, (i + 1) * hb // 2, term, 0)
+        for j in range(NJ):
+            d_copy(j, i).start()
 
     def add_to(dst, src, count):
         step = 8
@@ -234,19 +238,18 @@
         far, dev = (yq, ydev) if j % 2 == 0 else (xq, xdev)
         return rdma(part.at[c, j, far], r2.at[j], r2_s.at[j], r2_r.at[j], dev)
 
-    for j in range(NJ):
-        d_copy(j).wait()
-        near, far = (xq, yq) if j % 2 == 0 else (yq, xq)
+    def core_sum(j):
+        for i in range(2):
+            d_copy(j, i).wait()
+        for k in range(QUAD):
+            add_to(part.at[c, j, k], drecv.at[j, k], nblk)
+
+    def first_send(j):
         hops = first_hop(j)
-        add_to(part.at[c, j, dq], drecv.at[j, dq], nblk)
-        add_to(part.at[c, j, near], drecv.at[j, near], nblk)
         hops[1].start()
         hops[0].start()
-        add_to(part.at[c, j, far], drecv.at[j, far], nblk)
-        add_to(part.at[c, j, quad], drecv.at[j, quad], nblk)
-
-    ag_arrive(1)
-    for j in range(NJ):
+
+    def second_send(j):
         hops = first_hop(j)
         far = yq if j % 2 == 0 else xq
         hops[1].wait_recv()
@@ -330,16 +333,115 @@
         for cp in f_copies(j):
             cp.start()
 
-    for t in range(2, planes):
+    grp = 4
+    gw = grp * BLK
+
+    def weight_group(g):
+        return jnp.concatenate([whole[slot_of[g * grp + i]] for i in range(grp)], axis=0)
+
+    def fwd_body(g, carry):
+        cols = pl.ds(pl.multiple_of(g * gw, gw), gw)
+        normed = (tok[:, cols].astype(F32) * inv[...] * gain[:, cols]).astype(BF16)
+        fwd[...] += jnp.dot(normed, weight_group(g), preferred_element_type=F32)
+        return carry
+
+    def bwd_body(g, carry):
+        cols = pl.ds(pl.multiple_of(g * gw, gw), gw)
+        grad = lax.dot_general(
+            cot[...], weight_group(g), (((1,), (1,)), ((), ())), preferred_element_type=F32
+        )
+        values = tok[:, cols].astype(F32)
+        tgrad[:, cols] = (grad * gain[:, cols] * inv[...] - values * coef[...]).astype(BF16)
+        gst[0, :, cols] = jnp.sum(grad * values * inv[...], axis=0, keepdims=True) * scale
+        return carry
+
+    groups = nblk // grp
+    cuts = [0, groups // 2, groups]
+
+    def fwd_part(i):
+        lax.fori_loop(cuts[i], cuts[i + 1], fwd_body, 0)
+
+    def bwd_part(i):
+        lax.fori_loop(cuts[i], cuts[i + 1], bwd_body, 0)
+
+    def fwd_end():
+        total = fwd[...]
+        proj[...] = (total + bias[...]).astype(BF16)
+        inner = jnp.sum(total * cot[...].astype(F32), axis=1, keepdims=True) / width
+        coef[...] = inv[...] * inv[...] * inner
+
+    def g_copy(n):
+        dev = (partner, xdev, ydev)[n]
+        return rdma(gst.at[n], grecv.at[n], g_s.at[n], g_r.at[n], dev)
+
+    def g_step(n):
+        g_copy(n).wait_recv()
+        gst[n + 1] = gst[n] + grecv[n]
+        if n < 2:
+            g_copy(n + 1).start()
+
+    def gz_copy(d):
+        return rdma(gst.at[3], gz.at[z], gz_s.at[d - 1], gz_r.at[z], others[d - 1])
+
+    def gz_got(d):
+        q = (z + d) % planes
+        return rdma(gst.at[3], gz.at[q], gz_s.at[d - 1], gz_r.at[q], others[d - 1])
+
+    own_local.wait()
+    fwd[...] = jnp.zeros_like(fwd)
+    gst[0, :, width:] = jnp.sum(cot[...].astype(F32), axis=0, keepdims=True) * scale
+    early = list(range(NJ // 2))
+    late = list(range(NJ // 2, NJ))
+    for j in early:
+        core_sum(j)
+        first_send(j)
+    for j in late:
+        core_sum(j)
+    ag_arrive(1)
+    for j in early:
+        second_send(j)
+    for j in late:
+        first_send(j)
+    for t in range(2, planes - 1):
         ag_side(t - 1)
         ag_arrive(t)
-    for j in range(NJ):
+    for j in early:
         place(j)
-        for t in range(planes - 1):
+        z_step(j, 0)
+    for j in late:
+        second_send(j)
+    for j in early:
+        z_step(j, 1)
+    ag_side(planes - 2)
+    ag_arrive(planes - 1)
+    for j in late:
+        place(j)
+        z_step(j, 0)
+    for t in range(2, planes - 1):
+        for j in early:
             z_step(j, t)
+    for j in early:
+        z_end(j)
+    for j in late:
+        z_step(j, 1)
     ag_side(planes - 1)
-    for j in range(NJ):
+    for t in range(1, planes):
+        ag_finish(t)
+    own_partner.wait_send()
+    rdma(
+        w, span(2 * z + oc, 0, cap), agp_s.at[0, z], agp_r.at[0, z], partner
+    ).wait_recv()
+    fwd_part(0)
+    for t in range(2, planes - 1):
+        for j in late:
+            z_step(j, t)
+    fwd_part(1)
+    for j in late:
         z_end(j)
+    fwd_end()
+    bwd_part(0)
+    bwd_part(1)
+    g_copy(0).start()
 
     def f_got(j, n):
         ids = [quad * 2 + oc]
@@ -363,6 +465,23 @@
             return carry
 
         lax.fori_loop(0, cap, body, 0)
+        if j < 3:
+            g_step(j)
+        if j == 2:
+            gz[z] = gst[3]
+            for d in range(1, planes):
+                gz_copy(d).start()
+
+    for d in range(1, planes):
+        gz_got(d).wait_recv()
+    total = gz[0]
+    for q in range(1, planes):
+        total = total + gz[q]
+    vec[...] = total
+    for d in range(1, planes):
+        gz_copy(d).wait_send()
+    for n in range(3):
+        g_copy(n).wait_send()
 
     for j in range(NJ):
         for cp in first_hop(j):
@@ -379,13 +498,6 @@
             def _():
                 dn_copy(j, t).wait_send()
 
-    for t in range(1, planes):
-        ag_finish(t)
-    own_partner.wait_send()
-    from_partner_own = rdma(w, whole.at[2 * z + oc], agp_s.at[0, z], agp_r.at[0, z], partner)
-    from_partner_own.wait_recv()
-    own_local.wait()
-
     @pl.when(has_up)
     def _():
         own_z(0, updev).wait_send()
@@ -395,12 +507,12 @@
         own_z(1, dndev).wait_send()
 
 
-def communicate(tokens, norm_gain, cotangent, block_of_slot, key_weight, scale):
+def communicate(tokens, norm_gain, cotangent, key_bias, block_of_slot, block_slot, key_weight, scale):
     shard_count = lax.axis_size("shard")
     planes = shard_count // 2
     rows, cols = key_weight.shape
     cap = rows // BLK
-    width = tokens.shape[1]
+    tok_count, width = tokens.shape
     nblk = width // BLK
     group = cols // (2 * QUAD)
     dma = pltpu.SemaphoreType.DMA
@@ -408,19 +520,29 @@
     return pl.pallas_call(
         functools.partial(comm_kernel, planes, cap, nblk, scale),
         out_shape=(
-            jax.ShapeDtypeStruct((shard_count, rows, cols), BF16),
+            jax.ShapeDtypeStruct((tok_count, cols), BF16),
+            jax.ShapeDtypeStruct((tok_count, width), BF16),
             jax.ShapeDtypeStruct((rows, cols), F32),
+            jax.ShapeDtypeStruct((1, width + cols), F32),
         ),
         in_specs=[
             pl.BlockSpec(memory_space=vm),
             pl.BlockSpec(memory_space=vm),
             pl.BlockSpec(memory_space=vm),
+            pl.BlockSpec(memory_space=vm),
+            pl.BlockSpec(memory_space=pltpu.SMEM),
             pl.BlockSpec(memory_space=pltpu.SMEM),
             pl.BlockSpec(memory_space=vm),
         ],
-        out_specs=(pl.BlockSpec(memory_space=pl.ANY), pl.BlockSpec(memory_space=vm)),
+        out_specs=(pl.BlockSpec(memory_space=vm),) * 4,
         scratch_shapes=[
-            vm((tokens.shape[0], 1), F32),
+            vm((shard_count * cap, BLK, cols), BF16),
+            vm((tok_count, 1), F32),
+            vm((tok_count, 1), F32),
+            vm((tok_count, cols), F32),
+            vm((4, 1, width + cols), F32),
+            vm((3, 1, width + cols), F32),
+            vm((planes, 1, width + cols), F32),
             vm((2, NJ, QUAD, nblk, SUB, group), BF16),
             vm((NJ, QUAD, nblk, SUB, group), BF16),
             vm((NJ, 2, nblk, SUB, group), BF16),
@@ -435,17 +557,22 @@
             dma((planes,)), dma((planes,)),
             dma((planes,)), dma((planes,)),
             dma((4, planes)), dma((4, planes)),
-            dma((NJ,)), dma((NJ,)),
+            dma((NJ, 2)), dma((NJ, 2)),
             dma((NJ, 2)), dma((NJ, 2)),
             dma((NJ,)), dma((NJ,)),
             dma((NJ, planes)), dma((NJ, planes)),
             dma((NJ, planes)), dma((NJ, planes)),
             dma((NJ, 7)), dma((NJ, 8)),
+            dma((3,)), dma((3,)),
+            dma((planes,)), dma((planes,)),
         ],
         compiler_params=pltpu.CompilerParams(
-            collective_id=0, has_side_effects=True, vmem_limit_bytes=60 * 1024 * 1024
+            collective_id=0, has_side_effects=True, vmem_limit_bytes=67043328
         ),
-    )(tokens, norm_gain[None, :], cotangent, block_of_slot, key_weight)
+    )(
+        tokens, norm_gain[None, :], cotangent, key_bias[None, :], block_of_slot, block_slot,
+        key_weight.reshape(cap, BLK, cols),
+    )
 
 
 def local(tokens, norm_gain, key_bias, key_weight, cotangent, block_slot):
@@ -459,29 +586,13 @@
     match = block_slot[None, :] == jnp.arange(slot_total, dtype=jnp.int32)[:, None]
     numbers = jnp.arange(1, block_count + 1, dtype=jnp.int32)[None, :]
     block_of_slot = jnp.sum(jnp.where(match, numbers, 0), axis=1) - 1
-    whole, weight_grad = communicate(
-        tokens, norm_gain, cotangent, block_of_slot, key_weight, grad_scale
+    projected, token_grad, weight_grad, vec = communicate(
+        tokens, norm_gain, cotangent, key_bias, block_of_slot, block_slot, key_weight, grad_scale
     )
     if replicas > QUAD:
         groups = [list(range(i, replicas, QUAD)) for i in range(QUAD)]
-        weight_grad = lax.psum(weight_grad, "rep", axis_index_groups=groups)
-    weight = jnp.take(whole.reshape(slot_total, BLK, -1), block_slot, axis=0)
-    weight = weight.reshape(width, -1)
-    values = tokens.astype(F32)
-    inv_rms = lax.rsqrt(jnp.mean(values * values, axis=-1, keepdims=True) + EPS)
-    normed = (values * inv_rms * norm_gain).astype(BF16)
-    projected = jnp.dot(normed, weight, preferred_element_type=F32) + key_bias
-    projected = projected.astype(BF16)
-    grad_normed = lax.dot_general(
-        cotangent, weight, (((1,), (1,)), ((), ())), preferred_element_type=F32
-    )
-    scaled = grad_normed * norm_gain
-    inner = jnp.mean(scaled * values, axis=-1, keepdims=True)
-    token_grad = (inv_rms * (scaled - values * inv_rms * inv_rms * inner)).astype(BF16)
-    gain_part = jnp.sum(grad_normed * values * inv_rms, axis=0) * grad_scale
-    bias_part = jnp.sum(cotangent.astype(F32), axis=0) * grad_scale
-    gain_grad, bias_grad = lax.psum((gain_part, bias_part), ("shard", "rep"))
-    return (projected, token_grad, weight_grad, gain_grad, bias_grad)
+        weight_grad, vec = lax.psum((weight_grad, vec), "rep", axis_index_groups=groups)
+    return (projected, token_grad, weight_grad, vec[0, :width], vec[0, width:])
 
 
 def solution(mesh):

time: 273 us -> 166 us (0.61)
  blocking collectives: 47.1 us -> 0 us
  other arithmetic: 19.4 us -> 1.27 us
  local copies, waits for them, and re-layouts: 29 us -> 11.1 us
  matrix products: 17.2 us -> 0 us
  Pallas kernels: 159 us -> 153 us
    psum x1 -> x0, blocking collectives: 47.1 us -> none  [local(): gain_grad, bias_grad = lax.psum((gain_part, bias_part), ('shard', 'rep'))]
    dot_general x2 -> x0, matrix products: 17.2 us -> none  [the longest x1 10.5 us: local(): projected = jnp.dot(normed, weight, preferred_element_type=F32) + key_bias]
    gather x1 -> x0, local copies, waits for them, and re-layouts: 11.6 us -> none  [local(): weight = jnp.take(whole.reshape(slot_total, BLK, -1), block_slot, axis=0)]
    select_n x2 -> x0, other arithmetic: 10.8 us -> none  [local(): weight = jnp.take(whole.reshape(slot_total, BLK, -1), block_slot, axis=0)]
    unnamed x19 -> x5, local copies, waits for them, and re-layouts: 17.4 us -> 8.52 us
    pallas_call x1, Pallas kernels: 159 us -> 153 us  [communicate(): pl.pallas_call(functools.partial(comm_kernel, planes, cap, nblk, scale),...]
    convert_element_type x1 -> x0, other arithmetic: 3.92 us -> none  [local(): (inv_rms * (scaled - values * inv_rms * inv_rms * inner)).astype(BF16)]
    reduce_sum x2 -> x0, other arithmetic: 3.32 us -> none  [the longest x1 3.18 us: local(): inv_rms = lax.rsqrt(jnp.mean(values * values, axis=-1, keepdims=True) + EPS)]
where the time goes in v2:
time: 166 us
  Pallas kernels  153 us (92%)
  local copies, waits for them, and re-layouts  11.1 us (7%)
    pallas_call x1, Pallas kernels, communicate(): pl.pallas_call(functools.partial(comm_kernel, planes, cap, nblk, scale),...  153 us
    unnamed x5, local copies, waits for them, and re-layouts  8.52 us

profile of v2, /device:TPU:0, one launch (start us, length us, event | category | flops | bytes accessed | tf_op | source)
XLA Modules:
  0.0 166.1 jit_solution(16269594352273806643)
XLA Ops:
  0.6 0.7 select_reduce_fusion
  1.4 0.5 broadcast_add_fusion.bos
  1.9 153.0 %shard_map.101 = (bf16[384,1024]{1,0:T(8,128)(2,1)}, bf16[384,5120]{1,0:T(8,128)(2,1)}, f32[1024,1024]{1,0:T(8,128)}, f32[1,6144]{1,0:T(1,128)}) custom-call(bf16[384,5120]{1,0:T(8,128)(2,1)} %tok.1, f32[1,5120]{1,0:T(1,128)} %bitcast.7, bf16[384,1024]{1,0:T(8,128)(2,1)} %cot.1, f32[1,1024]{1,0:T(1,128)} %bitcast.9, s32[64]{0:T(128)} %broadcast_add_fusion.bos, ...), custom_call_target="tpu_custom_call" | custom-call | tf_op jit(solution)/shard_map/pallas_call | solution.py:520
  154.9 1.3 slice.7
  156.2 1.3 slice.6
  157.5 2.1 %copy.14 = bf16[384,1024]{1,0:T(8,128)(2,1)} copy(bf16[384,1024]{1,0:T(8,128)(2,1)} %get-tuple-element.18) | data formatting | bytes 1572864
  159.6 0.0 copy-start
  159.6 4.4 %copy.15 = bf16[384,5120]{1,0:T(8,128)(2,1)} copy(bf16[384,5120]{1,0:T(8,128)(2,1)} %get-tuple-element.19) | data formatting | bytes 7864320
  164.0 0.0 copy-done
  164.0 2.0 %copy.16 = f32[1024,1024]{1,0:T(8,128)} copy(f32[1024,1024]{1,0:T(8,128)S(1)} %copy-done) | data formatting | bytes 8388608
  (1 shorter events, 0.0 us)
Async XLA Ops:
  159.6 4.4 %copy-start = (f32[1024,1024]{1,0:T(8,128)S(1)}, f32[1024,1024]{1,0:T(8,128)}, u32[]{:S(2)}) copy-start(f32[1024,1024]{1,0:T(8,128)} %get-tuple-element.20) | copy-start | bytes 12582916

commit v3 on v2

--- a/solution.py
+++ b/solution.py
@@ -74,12 +74,16 @@
     other_x = ((1 - hh) * half, quar)
     other_y = ((1 - hh) * half + quar, quar)
 
-    def own_z(d, dev):
-        return rdma(w.at[pl.ds(*mine)], span(s, *mine), agz_s.at[d, z], agz_r.at[z], dev)
-
-    def fwd_z(q, d, dev):
-        ref = span(2 * q + c, *mine)
-        return rdma(ref, ref, agz_s.at[d, q], agz_r.at[q], dev)
+    piece = (mine_x, mine_y)
+
+    def own_z(d, i, dev):
+        return rdma(
+            w.at[pl.ds(*piece[i])], span(s, *piece[i]), agz_s.at[d, i, z], agz_r.at[i, z], dev
+        )
+
+    def fwd_z(q, d, i, dev):
+        ref = span(2 * q + c, *piece[i])
+        return rdma(ref, ref, agz_s.at[d, i, q], agz_r.at[i, q], dev)
 
     def fwd_x(q):
         ref = span(2 * q + c, *mine_x)
@@ -110,11 +114,13 @@
 
     @pl.when(has_up)
     def _():
-        own_z(0, updev).start()
+        own_z(0, 0, updev).start()
+        own_z(0, 1, updev).start()
 
     @pl.when(has_dn)
     def _():
-        own_z(1, dndev).start()
+        own_z(1, 0, dndev).start()
+        own_z(1, 1, dndev).start()
 
     own_partner.start()
     own_local.start()
@@ -128,22 +134,28 @@
         def _():
             f(z + t, 1)
 
-    def ag_arrive(t):
+    def ag_piece(t, i):
         def f(q, d):
-            fwd_z(q, d, updev).wait_recv()
+            fwd_z(q, d, i, updev).wait_recv()
             if d == 0:
                 @pl.when(has_up)
                 def _():
-                    fwd_z(q, 0, updev).start()
+                    fwd_z(q, 0, i, updev).start()
             else:
                 @pl.when(has_dn)
                 def _():
-                    fwd_z(q, 1, dndev).start()
-            fwd_x(q).start()
-            fwd_y(q).start()
-            to_partner(1, q, mine).start()
+                    fwd_z(q, 1, i, dndev).start()
+            if i == 0:
+                fwd_x(q).start()
+            else:
+                fwd_y(q).start()
+                to_partner(1, q, mine).start()
 
         each_foreign(t, f)
+
+    def ag_arrive(t):
+        ag_piece(t, 0)
+        ag_piece(t, 1)
 
     def ag_side(t):
         def f(q, d):
@@ -167,11 +179,13 @@
             if d == 0:
                 @pl.when(has_up)
                 def _():
-                    fwd_z(q, 0, updev).wait_send()
+                    fwd_z(q, 0, 0, updev).wait_send()
+                    fwd_z(q, 0, 1, updev).wait_send()
             else:
                 @pl.when(has_dn)
                 def _():
-                    fwd_z(q, 1, dndev).wait_send()
+                    fwd_z(q, 1, 0, dndev).wait_send()
+                    fwd_z(q, 1, 1, dndev).wait_send()
 
         each_foreign(t, f)
 
@@ -216,6 +230,7 @@
         lax.fori_loop(i * hb // 2, (i + 1) * hb // 2, term, 0)
         for j in range(NJ):
             d_copy(j, i).start()
+        ag_piece(1, i)
 
     def add_to(dst, src, count):
         step = 8
@@ -282,25 +297,30 @@
 
         lax.fori_loop(0, planes, body, 0)
 
+    def z_start(j):
+        @pl.when(z == 0)
+        def _():
+            for q in range(planes - 1, 0, -1):
+                up_copy(j, q).start()
+
+        @pl.when(z == planes - 1)
+        def _():
+            for q in range(planes - 1):
+                dn_copy(j, q).start()
+
     def z_step(j, t):
         qu = planes - 1 - t
 
-        @pl.when(z < qu)
-        def _():
-            @pl.when(has_dn)
-            def _():
-                up_copy(j, qu).wait_recv()
-                add_to(slots.at[j, qu], zup.at[j, qu], per_plane)
-
+        @pl.when(has_dn & (z < qu))
+        def _():
+            up_copy(j, qu).wait_recv()
+            add_to(slots.at[j, qu], zup.at[j, qu], per_plane)
             up_copy(j, qu).start()
 
-        @pl.when(z > t)
-        def _():
-            @pl.when(has_up)
-            def _():
-                dn_copy(j, t).wait_recv()
-                add_to(slots.at[j, t], zdn.at[j, t], per_plane)
-
+        @pl.when(has_up & (z > t))
+        def _():
+            dn_copy(j, t).wait_recv()
+            add_to(slots.at[j, t], zdn.at[j, t], per_plane)
             dn_copy(j, t).start()
 
     my_id = quad * 2 + c
@@ -397,7 +417,6 @@
         first_send(j)
     for j in late:
         core_sum(j)
-    ag_arrive(1)
     for j in early:
         second_send(j)
     for j in late:
@@ -407,6 +426,8 @@
         ag_arrive(t)
     for j in early:
         place(j)
+        z_start(j)
+    for j in early:
         z_step(j, 0)
     for j in late:
         second_send(j)
@@ -414,16 +435,17 @@
         z_step(j, 1)
     ag_side(planes - 2)
     ag_arrive(planes - 1)
-    for j in late:
-        place(j)
-        z_step(j, 0)
     for t in range(2, planes - 1):
         for j in early:
             z_step(j, t)
+    for j in late:
+        place(j)
+        z_start(j)
     for j in early:
         z_end(j)
-    for j in late:
-        z_step(j, 1)
+    for t in range(2):
+        for j in late:
+            z_step(j, t)
     ag_side(planes - 1)
     for t in range(1, planes):
         ag_finish(t)
@@ -435,9 +457,9 @@
     for t in range(2, planes - 1):
         for j in late:
             z_step(j, t)
-    fwd_part(1)
     for j in late:
         z_end(j)
+    fwd_part(1)
     fwd_end()
     bwd_part(0)
     bwd_part(1)
@@ -500,11 +522,13 @@
 
     @pl.when(has_up)
     def _():
-        own_z(0, updev).wait_send()
+        own_z(0, 0, updev).wait_send()
+        own_z(0, 1, updev).wait_send()
 
     @pl.when(has_dn)
     def _():
-        own_z(1, dndev).wait_send()
+        own_z(1, 0, dndev).wait_send()
+        own_z(1, 1, dndev).wait_send()
 
 
 def communicate(tokens, norm_gain, cotangent, key_bias, block_of_slot, block_slot, key_weight, scale):
@@ -553,7 +577,7 @@
             vm((NJ, 2 * cap, SUB, group), BF16),
             vm((2 * QUAD, NJ, cap, SUB, group), BF16),
             dma(()),
-            dma((2, planes)), dma((planes,)),
+            dma((2, 2, planes)), dma((2, planes)),
             dma((planes,)), dma((planes,)),
             dma((planes,)), dma((planes,)),
             dma((4, planes)), dma((4, planes)),

time: 166 us -> 171 us (1.030)
  Pallas kernels: 153 us -> 158 us
    pallas_call x1, Pallas kernels: 153 us -> 158 us  [communicate(): pl.pallas_call(functools.partial(comm_kernel, planes, cap, nblk, scale),...]
where the time goes in v3:
time: 171 us
  Pallas kernels  158 us (92%)
  local copies, waits for them, and re-layouts  11.1 us (6%)
    pallas_call x1, Pallas kernels, communicate(): pl.pallas_call(functools.partial(comm_kernel, planes, cap, nblk, scale),...  158 us
    unnamed x5, local copies, waits for them, and re-layouts  8.52 us

profile of v3, /device:TPU:0, one launch (start us, length us, event | category | flops | bytes accessed | tf_op | source)
XLA Modules:
  0.0 171.2 jit_solution(8650020149796046588)
XLA Ops:
  0.6 0.7 select_reduce_fusion
  1.4 0.5 broadcast_add_fusion.bos
  1.9 158.1 %shard_map.101 = (bf16[384,1024]{1,0:T(8,128)(2,1)}, bf16[384,5120]{1,0:T(8,128)(2,1)}, f32[1024,1024]{1,0:T(8,128)}, f32[1,6144]{1,0:T(1,128)}) custom-call(bf16[384,5120]{1,0:T(8,128)(2,1)} %tok.1, f32[1,5120]{1,0:T(1,128)} %bitcast.7, bf16[384,1024]{1,0:T(8,128)(2,1)} %cot.1, f32[1,1024]{1,0:T(1,128)} %bitcast.9, s32[64]{0:T(128)} %broadcast_add_fusion.bos, ...), custom_call_target="tpu_custom_call" | custom-call | tf_op jit(solution)/shard_map/pallas_call | solution.py:544
  160.0 1.3 slice.7
  161.3 1.3 slice.6
  162.6 2.1 %copy.14 = bf16[384,1024]{1,0:T(8,128)(2,1)} copy(bf16[384,1024]{1,0:T(8,128)(2,1)} %get-tuple-element.18) | data formatting | bytes 1572864
  164.7 0.0 copy-start
  164.7 4.4 %copy.15 = bf16[384,5120]{1,0:T(8,128)(2,1)} copy(bf16[384,5120]{1,0:T(8,128)(2,1)} %get-tuple-element.19) | data formatting | bytes 7864320
  169.1 0.0 copy-done
  169.1 2.0 %copy.16 = f32[1024,1024]{1,0:T(8,128)} copy(f32[1024,1024]{1,0:T(8,128)S(1)} %copy-done) | data formatting | bytes 8388608
  (1 shorter events, 0.0 us)
Async XLA Ops:
  164.7 4.4 %copy-start = (f32[1024,1024]{1,0:T(8,128)S(1)}, f32[1024,1024]{1,0:T(8,128)}, u32[]{:S(2)}) copy-start(f32[1024,1024]{1,0:T(8,128)} %get-tuple-element.20) | copy-start | bytes 12582916

commit v4 on v2

--- a/solution.py
+++ b/solution.py
@@ -159,6 +159,11 @@
             from_partner(1, q, mine).wait_recv()
             from_partner(2, q, other_x).wait_recv()
             from_partner(3, q, other_y).wait_recv()
+
+        each_foreign(t, f)
+
+    def ag_drain(t):
+        def f(q, d):
             to_partner(1, q, mine).wait_send()
             to_partner(2, q, other_x).wait_send()
             to_partner(3, q, other_y).wait_send()
@@ -282,25 +287,30 @@
 
         lax.fori_loop(0, planes, body, 0)
 
+    def z_start(chunks):
+        for t in range(planes - 1):
+            for j in chunks:
+                @pl.when(z == 0)
+                def _():
+                    up_copy(j, planes - 1 - t).start()
+
+                @pl.when(z == planes - 1)
+                def _():
+                    dn_copy(j, t).start()
+
     def z_step(j, t):
         qu = planes - 1 - t
 
-        @pl.when(z < qu)
+        @pl.when(has_dn & (z < qu))
         def _():
-            @pl.when(has_dn)
-            def _():
-                up_copy(j, qu).wait_recv()
-                add_to(slots.at[j, qu], zup.at[j, qu], per_plane)
-
+            up_copy(j, qu).wait_recv()
+            add_to(slots.at[j, qu], zup.at[j, qu], per_plane)
             up_copy(j, qu).start()
 
-        @pl.when(z > t)
+        @pl.when(has_up & (z > t))
         def _():
-            @pl.when(has_up)
-            def _():
-                dn_copy(j, t).wait_recv()
-                add_to(slots.at[j, t], zdn.at[j, t], per_plane)
-
+            dn_copy(j, t).wait_recv()
+            add_to(slots.at[j, t], zdn.at[j, t], per_plane)
             dn_copy(j, t).start()
 
     my_id = quad * 2 + c
@@ -407,6 +417,8 @@
         ag_arrive(t)
     for j in early:
         place(j)
+    z_start(early)
+    for j in early:
         z_step(j, 0)
     for j in late:
         second_send(j)
@@ -414,34 +426,43 @@
         z_step(j, 1)
     ag_side(planes - 2)
     ag_arrive(planes - 1)
-    for j in late:
-        place(j)
-        z_step(j, 0)
     for t in range(2, planes - 1):
         for j in early:
             z_step(j, t)
+    for j in late:
+        place(j)
+    z_start(late)
     for j in early:
         z_end(j)
-    for j in late:
-        z_step(j, 1)
     ag_side(planes - 1)
     for t in range(1, planes):
         ag_finish(t)
-    own_partner.wait_send()
     rdma(
         w, span(2 * z + oc, 0, cap), agp_s.at[0, z], agp_r.at[0, z], partner
     ).wait_recv()
     fwd_part(0)
-    for t in range(2, planes - 1):
+    for j in late:
+        z_step(j, 0)
+    fwd_part(1)
+    for t in range(1, planes - 1):
         for j in late:
             z_step(j, t)
-    fwd_part(1)
-    for j in late:
-        z_end(j)
+    middle = has_up & has_dn
+
+    @pl.when(middle)
+    def _():
+        for j in late:
+            z_end(j)
+
     fwd_end()
     bwd_part(0)
     bwd_part(1)
     g_copy(0).start()
+
+    @pl.when(jnp.logical_not(middle))
+    def _():
+        for j in late:
+            z_end(j)
 
     def f_got(j, n):
         ids = [quad * 2 + oc]
@@ -483,6 +504,9 @@
     for n in range(3):
         g_copy(n).wait_send()
 
+    for t in range(1, planes):
+        ag_drain(t)
+    own_partner.wait_send()
     for j in range(NJ):
         for cp in first_hop(j):
             cp.wait_send()

time: 166 us -> 169 us (1.018)
  Pallas kernels: 153 us -> 156 us
    pallas_call x1, Pallas kernels: 153 us -> 156 us  [communicate(): pl.pallas_call(functools.partial(comm_kernel, planes, cap, nblk, scale),...]
where the time goes in v4:
time: 169 us
  Pallas kernels  156 us (92%)
  local copies, waits for them, and re-layouts  11.1 us (7%)
    pallas_call x1, Pallas kernels, communicate(): pl.pallas_call(functools.partial(comm_kernel, planes, cap, nblk, scale),...  156 us
    unnamed x5, local copies, waits for them, and re-layouts  8.52 us

profile of v4, /device:TPU:0, one launch (start us, length us, event | category | flops | bytes accessed | tf_op | source)
XLA Modules:
  0.0 168.9 jit_solution(13118650777889176667)
XLA Ops:
  0.6 0.7 select_reduce_fusion
  1.4 0.5 broadcast_add_fusion.bos
  1.9 155.8 %shard_map.101 = (bf16[384,1024]{1,0:T(8,128)(2,1)}, bf16[384,5120]{1,0:T(8,128)(2,1)}, f32[1024,1024]{1,0:T(8,128)}, f32[1,6144]{1,0:T(1,128)}) custom-call(bf16[384,5120]{1,0:T(8,128)(2,1)} %tok.1, f32[1,5120]{1,0:T(1,128)} %bitcast.7, bf16[384,1024]{1,0:T(8,128)(2,1)} %cot.1, f32[1,1024]{1,0:T(1,128)} %bitcast.9, s32[64]{0:T(128)} %broadcast_add_fusion.bos, ...), custom_call_target="tpu_custom_call" | custom-call | tf_op jit(solution)/shard_map/pallas_call | solution.py:544
  157.8 1.3 slice.7
  159.0 1.3 slice.6
  160.4 2.1 %copy.14 = bf16[384,1024]{1,0:T(8,128)(2,1)} copy(bf16[384,1024]{1,0:T(8,128)(2,1)} %get-tuple-element.18) | data formatting | bytes 1572864
  162.4 0.0 copy-start
  162.4 4.4 %copy.15 = bf16[384,5120]{1,0:T(8,128)(2,1)} copy(bf16[384,5120]{1,0:T(8,128)(2,1)} %get-tuple-element.19) | data formatting | bytes 7864320
  166.9 0.0 copy-done
  166.9 2.0 %copy.16 = f32[1024,1024]{1,0:T(8,128)} copy(f32[1024,1024]{1,0:T(8,128)S(1)} %copy-done) | data formatting | bytes 8388608
  (1 shorter events, 0.0 us)
Async XLA Ops:
  162.4 4.4 %copy-start = (f32[1024,1024]{1,0:T(8,128)S(1)}, f32[1024,1024]{1,0:T(8,128)}, u32[]{:S(2)}) copy-start(f32[1024,1024]{1,0:T(8,128)} %get-tuple-element.20) | copy-start | bytes 12582916
